TPU v7x, 32 devices: a whole 2x2x4 slice. The times are simulated.
32 devices in a mesh: row: 8 (over y, x, core), col: 4 (over z).
Axes of the slice: x: 2, y: 2, z: 4, core: 2. Of those that a mesh axis runs over, the one named last changes fastest.
Arguments:
- singular_vectors: float32 [4096, 4096], P('row', 'col'), may hold values from -6 to 6
- reflector_vectors: float32 [2, 16, 256, 512], P(None, 'row', 'col'), may hold values from -2 to 2, as said below
- reflector_factors: float32 [2, 16, 256, 256], P(None, 'row', 'col'), as said below
- sweep_bounds: int32 [2, 2], replicated, may hold values from 0 to 3584, as said below
Outputs:
- transformed: float32 [4096, 4096], P('row', 'col')
Inputs may be any that keep to these rules, and one draw needn't show every extreme that they name: `reflector_vectors`: row j of each block's 256 x 2 * 256 slice is a reflector: 1 at position j, nonzero only at positions j to j + 255. `reflector_factors`: each block's factor is the upper triangular inverse of the strictly upper part of W W^T plus half of its diagonal, W being that block's slice of reflector_vectors, so that each block's transformation is orthogonal. `sweep_bounds`: both entries are multiples of 256, and the first is below the second.
All inputs are finite; a program needn't handle non-finite values.
Results may differ from a plain program's by a relative error of at most 0.0003.
Values sent between devices are 32-bit elements; how exact they have to be, the bound alone decides.
A program may use at most 64 MiB of HBM per device.

v0:
```python
import jax
import jax.numpy as jnp
from jax import lax
from jax.sharding import PartitionSpec as P

exact_mode = lax.Precision.HIGHEST


def extended_2(block, sides, width):
    for axis, dim in sides:
        count = lax.axis_size(axis)
        forward = [(i, i + 1) for i in range(count - 1)]
        backward = [(target, source) for source, target in forward]
        low = lax.ppermute(
            lax.slice_in_dim(block, block.shape[dim] - width, None, axis=dim), axis, forward
        )
        high = lax.ppermute(lax.slice_in_dim(block, 0, width, axis=dim), axis, backward)
        block = jnp.concatenate([low, block, high], axis=dim)
    return block


def apply_block(row_block, vectors, factor):
    inner_part = jnp.dot(
        vectors, row_block, precision=exact_mode, preferred_element_type=jnp.float32
    )
    inner_part = jnp.dot(
        factor, inner_part, precision=exact_mode, preferred_element_type=jnp.float32
    )
    return row_block - jnp.dot(
        vectors.T, inner_part, precision=exact_mode, preferred_element_type=jnp.float32
    )


def keep_same(operand):
    return operand


def per_device(singular_vectors, reflector_vectors, reflector_factors, sweep_bounds):
    row_count = lax.axis_size("row")
    owner_row = lax.axis_index("row")
    row_dev, col_count = singular_vectors.shape
    reflect = reflector_vectors.shape[3] // 2
    blocks_dev = row_dev // reflect
    sweep_count = reflector_vectors.shape[0]
    vectors_all, factors_all = (
        lax.all_gather(reflector_vectors, "col", axis=2, tiled=True),
        lax.all_gather(reflector_factors, "col", axis=2, tiled=True),
    )
    pieces = 4
    piece_cols = col_count // pieces
    unit_count = sweep_count * pieces
    steps_total = row_count - 1 + unit_count
    lag_steps = row_count - 1 - owner_row

    def one_step(step_id, state_pair):
        field_now, below_rows = state_pair
        unit_now = step_id - lag_steps
        active = (unit_now >= 0) & (unit_now < unit_count)
        unit_safe = jnp.clip(unit_now, 0, unit_count - 1)
        col_start = unit_safe % pieces * piece_cols
        sweep_id = unit_safe // pieces
        first_row = sweep_bounds[sweep_id, 0]
        last_row = sweep_bounds[sweep_id, 1]
        vec_sweep = lax.dynamic_index_in_dim(vectors_all, sweep_id, 0, keepdims=False)
        fac_sweep = lax.dynamic_index_in_dim(factors_all, sweep_id, 0, keepdims=False)

        def work(operand):
            field_in, below_in = operand
            own_part = lax.dynamic_slice_in_dim(field_in, col_start, piece_cols, 1)
            extended = jnp.concatenate([own_part, below_in], axis=0)

            def one_block(counter, current):
                local_id = blocks_dev - 1 - counter
                start_row = (owner_row * blocks_dev + local_id) * reflect
                is_live = (start_row >= first_row) & (start_row <= last_row)

                def update(matrix):
                    row_block = lax.dynamic_slice_in_dim(matrix, local_id * reflect, 2 * reflect, 0)
                    vectors = lax.dynamic_index_in_dim(vec_sweep, local_id, 0, keepdims=False)
                    factor = lax.dynamic_index_in_dim(fac_sweep, local_id, 0, keepdims=False)
                    row_block = apply_block(row_block, vectors, factor)
                    return lax.dynamic_update_slice_in_dim(matrix, row_block, local_id * reflect, 0)

                return lax.cond(is_live, update, keep_same, current)

            extended = lax.fori_loop(0, blocks_dev, one_block, extended)
            field_out = lax.dynamic_update_slice_in_dim(field_in, extended[:row_dev], col_start, 1)
            return (field_out, extended[row_dev:])

        field_now, returned = lax.cond(active, work, keep_same, (field_now, below_rows))
        top_rows = lax.dynamic_slice(field_now, (0, col_start), (reflect, piece_cols))
        message = jnp.concatenate([top_rows, returned], axis=0)
        padded = extended_2(message, (("row", 0),), reflect)
        from_left = padded[:reflect]
        below_next = padded[3 * reflect :]
        prior = unit_now - 1
        valid = (owner_row > 0) & (prior >= 0) & (prior < unit_count)
        prior_col = jnp.clip(prior, 0, unit_count - 1) % pieces * piece_cols
        current_top = lax.dynamic_slice(field_now, (0, prior_col), (reflect, piece_cols))
        field_now = lax.dynamic_update_slice(
            field_now, jnp.where(valid, from_left, current_top), (0, prior_col)
        )
        return (field_now, below_next)

    def two_steps(pair_id, state_pair):
        return one_step(2 * pair_id + 1, one_step(2 * pair_id, state_pair))

    below_start = jnp.zeros((reflect, piece_cols), jnp.float32)
    pair_count = (steps_total + 1) // 2
    result_field, below_last = lax.fori_loop(
        0, pair_count, two_steps, (singular_vectors, below_start)
    )
    return result_field


def solution(mesh):
    placed = (P("row", "col"), P(None, "row", "col", None), P(None, "row", "col", None), P())
    return jax.shard_map(
        per_device, mesh=mesh, in_specs=placed, out_specs=P("row", "col"), check_vma=False
    )
```

profile of v0, /device:TPU:0, one launch (start us, length us, event | category | flops | bytes accessed | tf_op | source)
XLA Modules:
  0.0 520.1 jit_solution(4495330475815302078)
XLA Ops:
  10.5 30.1 %all-gather.5.cloned.1.call-done = f32[2,2,256,256]{3,2,1,0:T(8,128)} async-done(((f32[2,2,64,256]{3,2,1,0:T(8,128)}), f32[2,2,256,256]{3,2,1,0:T(8,128)}) %all-gather.5.cloned.1.call-update) | async-done | bytes 1048592 | tf_op jit(solution)/shard_map/all_gather | solution.py:47
  40.6 46.6 %all-gather.3.cloned.1.call-done = f32[2,2,256,512]{3,2,1,0:T(8,128)} async-done(((f32[2,2,64,512]{3,2,1,0:T(8,128)}), f32[2,2,256,512]{3,2,1,0:T(8,128)}) %all-gather.3.cloned.1.call-update) | async-done | bytes 2097168 | tf_op jit(solution)/shard_map/all_gather | solution.py:46
  87.3 426.0 %while.66 = (s32[]{:T(128)}, f32[512,1024]{1,0:T(8,128)}, f32[256,256]{1,0:T(8,128)S(1)}, s32[]{:T(128)}, s32[2,2]{1,0:T(2,128)S(1)}, /*index=5*/f32[2,2,256,512...) while((s32[]{:T(128)}, f32[512,1024]{1,0:T(8,128)}, ...), condition=%wide.region_13.14_spmd, body=%wide.region_0.13_spmd.sunk | while | flops 2014052352 | bytes 39848304 | solution.py:110
  141.3 13.3 %collective-permute-done.3 = f32[256,256]{1,0:T(8,128)S(1)} collective-permute-done((f32[256,256]{1,0:T(8,128)S(1)}, f32[256,256]{1,0:T(8,128)S(1)}, u32[]{:S(2)}, u32[]{:S(2)}) %collective-permute-start.3) | collective-permute-done | bytes 262176 | tf_op jit(solution)/shard_map/while/body/eval_jaxpr/ppermute | solution.py:17
  154.6 22.5 %collective-permute-start = (f32[256,256]{1,0:T(8,128)S(1)}, f32[256,256]{1,0:T(8,128)S(1)}, u32[]{:S(2)}, u32[]{:S(2)}) collective-permute-start(f32[256,256]{1,0:T(8,128)S(1)} %get-tuple-element.1131), channel_id=1, source_target_pairs={{0,4},{4,8},{8,12},{12,16},{16,20},{20,24},{24,28},{1,5},{5,9},{9,... | collective-permute-start | bytes 786440 | tf_op jit(solution)/shard_map/while/body/eval_jaxpr/ppermute | solution.py:14
  181.3 16.1 %collective-permute-done.1 = f32[256,256]{1,0:T(8,128)S(1)} collective-permute-done((f32[256,256]{1,0:T(8,128)S(1)}, f32[256,256]{1,0:T(8,128)S(1)}, u32[]{:S(2)}, u32[]{:S(2)}) %collective-permute-start.1) | collective-permute-done | bytes 262176 | tf_op jit(solution)/shard_map/while/body/eval_jaxpr/ppermute | solution.py:17
  197.4 22.5 %collective-permute-start.2 = (f32[256,256]{1,0:T(8,128)S(1)}, f32[256,256]{1,0:T(8,128)S(1)}, u32[]{:S(2)}, u32[]{:S(2)}) collective-permute-start(f32[256,256]{1,0:T(8,128)S(1)} %get-tuple-element.1135), channel_id=1, source_target_pairs={{0,4},{4,8},{8,12},{12,16},{16,20},{20,24},{24,28},{1,5},{5,9},{9,... | collective-permute-start | bytes 786440 | tf_op jit(solution)/shard_map/while/body/eval_jaxpr/ppermute | solution.py:14
  224.1 16.9 %collective-permute-done.3 = f32[256,256]{1,0:T(8,128)S(1)} collective-permute-done((f32[256,256]{1,0:T(8,128)S(1)}, f32[256,256]{1,0:T(8,128)S(1)}, u32[]{:S(2)}, u32[]{:S(2)}) %collective-permute-start.3) | collective-permute-done | bytes 262176 | tf_op jit(solution)/shard_map/while/body/eval_jaxpr/ppermute | solution.py:17
  241.0 21.8 %collective-permute-start = (f32[256,256]{1,0:T(8,128)S(1)}, f32[256,256]{1,0:T(8,128)S(1)}, u32[]{:S(2)}, u32[]{:S(2)}) collective-permute-start(f32[256,256]{1,0:T(8,128)S(1)} %get-tuple-element.1131), channel_id=1, source_target_pairs={{0,4},{4,8},{8,12},{12,16},{16,20},{20,24},{24,28},{1,5},{5,9},{9,... | collective-permute-start | bytes 786440 | tf_op jit(solution)/shard_map/while/body/eval_jaxpr/ppermute | solution.py:14
  270.8 9.2 %conditional.9 = ((f32[512,1024]{1,0:T(8,128)}, f32[256,256]{1,0:T(8,128)S(1)})) conditional(s32[]{:T(128)} %convert_element_type.44, (f32[512,1024]{1,0:T(8,128)}, f32[256,256]{1,0:T(8,128)S(1)}) %tuple.173, (s32[]{:T(128)}, f32[512,1024]{1,0:T(8,128)}, f32[256,256]{1,0:T(8,128)S(1)}, s32[]{:T(128)}, pred[]{:T(512)}, ...), branch_computations={%region_7.7_spmd, %region_8.12_spmd} | conditional | flops 1006960640 | bytes 16515680 | solution.py:90
  280.0 12.4 %collective-permute-start.2 = (f32[256,256]{1,0:T(8,128)S(1)}, f32[256,256]{1,0:T(8,128)S(1)}, u32[]{:S(2)}, u32[]{:S(2)}) collective-permute-start(f32[256,256]{1,0:T(8,128)S(1)} %get-tuple-element.1135), channel_id=1, source_target_pairs={{0,4},{4,8},{8,12},{12,16},{16,20},{20,24},{24,28},{1,5},{5,9},{9,... | collective-permute-start | bytes 786440 | tf_op jit(solution)/shard_map/while/body/eval_jaxpr/ppermute | solution.py:14
  300.5 9.2 %conditional.8 = ((f32[512,1024]{1,0:T(8,128)}, f32[256,256]{1,0:T(8,128)S(1)})) conditional(s32[]{:T(128)} %convert_element_type.45, (f32[512,1024]{1,0:T(8,128)}, f32[256,256]{1,0:T(8,128)S(1)}) %tuple.171, (s32[]{:T(128)}, f32[512,1024]{1,0:T(8,128)}, f32[256,256]{1,0:T(8,128)S(1)}, s32[]{:T(128)}, pred[]{:T(512)}, ...), branch_computations={%region_1.1_spmd, %region_2.6_spmd} | conditional | flops 1006960640 | bytes 16515680 | solution.py:90
  309.7 11.7 %collective-permute-start = (f32[256,256]{1,0:T(8,128)S(1)}, f32[256,256]{1,0:T(8,128)S(1)}, u32[]{:S(2)}, u32[]{:S(2)}) collective-permute-start(f32[256,256]{1,0:T(8,128)S(1)} %get-tuple-element.1131), channel_id=1, source_target_pairs={{0,4},{4,8},{8,12},{12,16},{16,20},{20,24},{24,28},{1,5},{5,9},{9,... | collective-permute-start | bytes 786440 | tf_op jit(solution)/shard_map/while/body/eval_jaxpr/ppermute | solution.py:14
  329.4 9.2 %conditional.9 = ((f32[512,1024]{1,0:T(8,128)}, f32[256,256]{1,0:T(8,128)S(1)})) conditional(s32[]{:T(128)} %convert_element_type.44, (f32[512,1024]{1,0:T(8,128)}, f32[256,256]{1,0:T(8,128)S(1)}) %tuple.173, (s32[]{:T(128)}, f32[512,1024]{1,0:T(8,128)}, f32[256,256]{1,0:T(8,128)S(1)}, s32[]{:T(128)}, pred[]{:T(512)}, ...), branch_computations={%region_7.7_spmd, %region_8.12_spmd} | conditional | flops 1006960640 | bytes 16515680 | solution.py:90
  338.6 12.3 %collective-permute-start.2 = (f32[256,256]{1,0:T(8,128)S(1)}, f32[256,256]{1,0:T(8,128)S(1)}, u32[]{:S(2)}, u32[]{:S(2)}) collective-permute-start(f32[256,256]{1,0:T(8,128)S(1)} %get-tuple-element.1135), channel_id=1, source_target_pairs={{0,4},{4,8},{8,12},{12,16},{16,20},{20,24},{24,28},{1,5},{5,9},{9,... | collective-permute-start | bytes 786440 | tf_op jit(solution)/shard_map/while/body/eval_jaxpr/ppermute | solution.py:14
  359.4 8.5 %conditional.8 = ((f32[512,1024]{1,0:T(8,128)}, f32[256,256]{1,0:T(8,128)S(1)})) conditional(s32[]{:T(128)} %convert_element_type.45, (f32[512,1024]{1,0:T(8,128)}, f32[256,256]{1,0:T(8,128)S(1)}) %tuple.171, (s32[]{:T(128)}, f32[512,1024]{1,0:T(8,128)}, f32[256,256]{1,0:T(8,128)S(1)}, s32[]{:T(128)}, pred[]{:T(512)}, ...), branch_computations={%region_1.1_spmd, %region_2.6_spmd} | conditional | flops 1006960640 | bytes 16515680 | solution.py:90
  367.9 13.3 %collective-permute-start = (f32[256,256]{1,0:T(8,128)S(1)}, f32[256,256]{1,0:T(8,128)S(1)}, u32[]{:S(2)}, u32[]{:S(2)}) collective-permute-start(f32[256,256]{1,0:T(8,128)S(1)} %get-tuple-element.1131), channel_id=1, source_target_pairs={{0,4},{4,8},{8,12},{12,16},{16,20},{20,24},{24,28},{1,5},{5,9},{9,... | collective-permute-start | bytes 786440 | tf_op jit(solution)/shard_map/while/body/eval_jaxpr/ppermute | solution.py:14
  389.2 13.3 %conditional.9 = ((f32[512,1024]{1,0:T(8,128)}, f32[256,256]{1,0:T(8,128)S(1)})) conditional(s32[]{:T(128)} %convert_element_type.44, (f32[512,1024]{1,0:T(8,128)}, f32[256,256]{1,0:T(8,128)S(1)}) %tuple.173, (s32[]{:T(128)}, f32[512,1024]{1,0:T(8,128)}, f32[256,256]{1,0:T(8,128)S(1)}, s32[]{:T(128)}, pred[]{:T(512)}, ...), branch_computations={%region_7.7_spmd, %region_8.12_spmd} | conditional | flops 1006960640 | bytes 16515680 | solution.py:90
  402.5 8.3 %collective-permute-start.2 = (f32[256,256]{1,0:T(8,128)S(1)}, f32[256,256]{1,0:T(8,128)S(1)}, u32[]{:S(2)}, u32[]{:S(2)}) collective-permute-start(f32[256,256]{1,0:T(8,128)S(1)} %get-tuple-element.1135), channel_id=1, source_target_pairs={{0,4},{4,8},{8,12},{12,16},{16,20},{20,24},{24,28},{1,5},{5,9},{9,... | collective-permute-start | bytes 786440 | tf_op jit(solution)/shard_map/while/body/eval_jaxpr/ppermute | solution.py:14
  418.9 13.3 %conditional.8 = ((f32[512,1024]{1,0:T(8,128)}, f32[256,256]{1,0:T(8,128)S(1)})) conditional(s32[]{:T(128)} %convert_element_type.45, (f32[512,1024]{1,0:T(8,128)}, f32[256,256]{1,0:T(8,128)S(1)}) %tuple.171, (s32[]{:T(128)}, f32[512,1024]{1,0:T(8,128)}, f32[256,256]{1,0:T(8,128)S(1)}, s32[]{:T(128)}, pred[]{:T(512)}, ...), branch_computations={%region_1.1_spmd, %region_2.6_spmd} | conditional | flops 1006960640 | bytes 16515680 | solution.py:90
  432.2 7.6 %collective-permute-start = (f32[256,256]{1,0:T(8,128)S(1)}, f32[256,256]{1,0:T(8,128)S(1)}, u32[]{:S(2)}, u32[]{:S(2)}) collective-permute-start(f32[256,256]{1,0:T(8,128)S(1)} %get-tuple-element.1131), channel_id=1, source_target_pairs={{0,4},{4,8},{8,12},{12,16},{16,20},{20,24},{24,28},{1,5},{5,9},{9,... | collective-permute-start | bytes 786440 | tf_op jit(solution)/shard_map/while/body/eval_jaxpr/ppermute | solution.py:14
  447.8 13.3 %conditional.9 = ((f32[512,1024]{1,0:T(8,128)}, f32[256,256]{1,0:T(8,128)S(1)})) conditional(s32[]{:T(128)} %convert_element_type.44, (f32[512,1024]{1,0:T(8,128)}, f32[256,256]{1,0:T(8,128)S(1)}) %tuple.173, (s32[]{:T(128)}, f32[512,1024]{1,0:T(8,128)}, f32[256,256]{1,0:T(8,128)S(1)}, s32[]{:T(128)}, pred[]{:T(512)}, ...), branch_computations={%region_7.7_spmd, %region_8.12_spmd} | conditional | flops 1006960640 | bytes 16515680 | solution.py:90
  475.9 12.6 %conditional.8 = ((f32[512,1024]{1,0:T(8,128)}, f32[256,256]{1,0:T(8,128)S(1)})) conditional(s32[]{:T(128)} %convert_element_type.45, (f32[512,1024]{1,0:T(8,128)}, f32[256,256]{1,0:T(8,128)S(1)}) %tuple.171, (s32[]{:T(128)}, f32[512,1024]{1,0:T(8,128)}, f32[256,256]{1,0:T(8,128)S(1)}, s32[]{:T(128)}, pred[]{:T(512)}, ...), branch_computations={%region_1.1_spmd, %region_2.6_spmd} | conditional | flops 1006960640 | bytes 16515680 | solution.py:90
  496.1 9.2 %collective-permute-start.2 = (f32[256,256]{1,0:T(8,128)S(1)}, f32[256,256]{1,0:T(8,128)S(1)}, u32[]{:S(2)}, u32[]{:S(2)}) collective-permute-start(f32[256,256]{1,0:T(8,128)S(1)} %get-tuple-element.1135), channel_id=1, source_target_pairs={{0,4},{4,8},{8,12},{12,16},{16,20},{20,24},{24,28},{1,5},{5,9},{9,... | collective-permute-start | bytes 786440 | tf_op jit(solution)/shard_map/while/body/eval_jaxpr/ppermute | solution.py:14
  (211 shorter events, 273.3 us)
Async XLA Ops:
  6.5 34.1 %all-gather.5.cloned.1.call-start = ((), (), s32[]{:S(2)}) async-start(), calls=%async_computation.1 | async-start | bytes 1310720 | tf_op jit(solution)/shard_map/all_gather | solution.py:47
  9.7 77.5 %all-gather.3.cloned.1.call-start = ((), (), s32[]{:S(2)}) async-start(), calls=%async_computation | async-start | bytes 2621440 | tf_op jit(solution)/shard_map/all_gather | solution.py:46
  91.8 7.0 %collective-permute-start.1 = (f32[256,256]{1,0:T(8,128)S(1)}, f32[256,256]{1,0:T(8,128)S(1)}, u32[]{:S(2)}, u32[]{:S(2)}) collective-permute-start(f32[256,256]{1,0:T(8,128)S(1)} %get-tuple-element.1133), channel_id=1, source_target_pairs={{4,0},{8,4},{12,8},{16,12},{20,16},{24,20},{28,24},{5,1},{9,5},{13... | collective-permute-start | bytes 786440 | tf_op jit(solution)/shard_map/while/body/eval_jaxpr/ppermute | solution.py:17
  98.8 8.6 %collective-permute-start.2 = (f32[256,256]{1,0:T(8,128)S(1)}, f32[256,256]{1,0:T(8,128)S(1)}, u32[]{:S(2)}, u32[]{:S(2)}) collective-permute-start(f32[256,256]{1,0:T(8,128)S(1)} %get-tuple-element.1135), channel_id=1, source_target_pairs={{0,4},{4,8},{8,12},{12,16},{16,20},{20,24},{24,28},{1,5},{5,9},{9,... | collective-permute-start | bytes 786440 | tf_op jit(solution)/shard_map/while/body/eval_jaxpr/ppermute | solution.py:14
  109.2 5.1 collective-permute-start.3
  114.2 8.6 %collective-permute-start = (f32[256,256]{1,0:T(8,128)S(1)}, f32[256,256]{1,0:T(8,128)S(1)}, u32[]{:S(2)}, u32[]{:S(2)}) collective-permute-start(f32[256,256]{1,0:T(8,128)S(1)} %get-tuple-element.1131), channel_id=1, source_target_pairs={{0,4},{4,8},{8,12},{12,16},{16,20},{20,24},{24,28},{1,5},{5,9},{9,... | collective-permute-start | bytes 786440 | tf_op jit(solution)/shard_map/while/body/eval_jaxpr/ppermute | solution.py:14
  129.7 8.6 %collective-permute-start.2 = (f32[256,256]{1,0:T(8,128)S(1)}, f32[256,256]{1,0:T(8,128)S(1)}, u32[]{:S(2)}, u32[]{:S(2)}) collective-permute-start(f32[256,256]{1,0:T(8,128)S(1)} %get-tuple-element.1135), channel_id=1, source_target_pairs={{0,4},{4,8},{8,12},{12,16},{16,20},{20,24},{24,28},{1,5},{5,9},{9,... | collective-permute-start | bytes 786440 | tf_op jit(solution)/shard_map/while/body/eval_jaxpr/ppermute | solution.py:14
  140.0 14.6 %collective-permute-start.3 = (f32[256,256]{1,0:T(8,128)S(1)}, f32[256,256]{1,0:T(8,128)S(1)}, u32[]{:S(2)}, u32[]{:S(2)}) collective-permute-start(f32[256,256]{1,0:T(8,128)S(1)} %get-tuple-element.1137), channel_id=1, source_target_pairs={{4,0},{8,4},{12,8},{16,12},{20,16},{24,20},{28,24},{5,1},{9,5},{13... | collective-permute-start | bytes 786440 | tf_op jit(solution)/shard_map/while/body/eval_jaxpr/ppermute | solution.py:17
  154.6 23.6 %collective-permute-start = (f32[256,256]{1,0:T(8,128)S(1)}, f32[256,256]{1,0:T(8,128)S(1)}, u32[]{:S(2)}, u32[]{:S(2)}) collective-permute-start(f32[256,256]{1,0:T(8,128)S(1)} %get-tuple-element.1131), channel_id=1, source_target_pairs={{0,4},{4,8},{8,12},{12,16},{16,20},{20,24},{24,28},{1,5},{5,9},{9,... | collective-permute-start | bytes 786440 | tf_op jit(solution)/shard_map/while/body/eval_jaxpr/ppermute | solution.py:14
  180.0 17.4 %collective-permute-start.1 = (f32[256,256]{1,0:T(8,128)S(1)}, f32[256,256]{1,0:T(8,128)S(1)}, u32[]{:S(2)}, u32[]{:S(2)}) collective-permute-start(f32[256,256]{1,0:T(8,128)S(1)} %get-tuple-element.1133), channel_id=1, source_target_pairs={{4,0},{8,4},{12,8},{16,12},{20,16},{24,20},{28,24},{5,1},{9,5},{13... | collective-permute-start | bytes 786440 | tf_op jit(solution)/shard_map/while/body/eval_jaxpr/ppermute | solution.py:17
  197.4 23.6 %collective-permute-start.2 = (f32[256,256]{1,0:T(8,128)S(1)}, f32[256,256]{1,0:T(8,128)S(1)}, u32[]{:S(2)}, u32[]{:S(2)}) collective-permute-start(f32[256,256]{1,0:T(8,128)S(1)} %get-tuple-element.1135), channel_id=1, source_target_pairs={{0,4},{4,8},{8,12},{12,16},{16,20},{20,24},{24,28},{1,5},{5,9},{9,... | collective-permute-start | bytes 786440 | tf_op jit(solution)/shard_map/while/body/eval_jaxpr/ppermute | solution.py:14
  222.8 18.2 %collective-permute-start.3 = (f32[256,256]{1,0:T(8,128)S(1)}, f32[256,256]{1,0:T(8,128)S(1)}, u32[]{:S(2)}, u32[]{:S(2)}) collective-permute-start(f32[256,256]{1,0:T(8,128)S(1)} %get-tuple-element.1137), channel_id=1, source_target_pairs={{4,0},{8,4},{12,8},{16,12},{20,16},{24,20},{28,24},{5,1},{9,5},{13... | collective-permute-start | bytes 786440 | tf_op jit(solution)/shard_map/while/body/eval_jaxpr/ppermute | solution.py:17
  241.0 22.9 %collective-permute-start = (f32[256,256]{1,0:T(8,128)S(1)}, f32[256,256]{1,0:T(8,128)S(1)}, u32[]{:S(2)}, u32[]{:S(2)}) collective-permute-start(f32[256,256]{1,0:T(8,128)S(1)} %get-tuple-element.1131), channel_id=1, source_target_pairs={{0,4},{4,8},{8,12},{12,16},{16,20},{20,24},{24,28},{1,5},{5,9},{9,... | collective-permute-start | bytes 786440 | tf_op jit(solution)/shard_map/while/body/eval_jaxpr/ppermute | solution.py:14
  265.7 5.1 collective-permute-start.1
  280.0 13.6 %collective-permute-start.2 = (f32[256,256]{1,0:T(8,128)S(1)}, f32[256,256]{1,0:T(8,128)S(1)}, u32[]{:S(2)}, u32[]{:S(2)}) collective-permute-start(f32[256,256]{1,0:T(8,128)S(1)} %get-tuple-element.1135), channel_id=1, source_target_pairs={{0,4},{4,8},{8,12},{12,16},{16,20},{20,24},{24,28},{1,5},{5,9},{9,... | collective-permute-start | bytes 786440 | tf_op jit(solution)/shard_map/while/body/eval_jaxpr/ppermute | solution.py:14
  295.4 5.1 collective-permute-start.3
  309.7 12.9 %collective-permute-start = (f32[256,256]{1,0:T(8,128)S(1)}, f32[256,256]{1,0:T(8,128)S(1)}, u32[]{:S(2)}, u32[]{:S(2)}) collective-permute-start(f32[256,256]{1,0:T(8,128)S(1)} %get-tuple-element.1131), channel_id=1, source_target_pairs={{0,4},{4,8},{8,12},{12,16},{16,20},{20,24},{24,28},{1,5},{5,9},{9,... | collective-permute-start | bytes 786440 | tf_op jit(solution)/shard_map/while/body/eval_jaxpr/ppermute | solution.py:14
  338.6 13.4 %collective-permute-start.2 = (f32[256,256]{1,0:T(8,128)S(1)}, f32[256,256]{1,0:T(8,128)S(1)}, u32[]{:S(2)}, u32[]{:S(2)}) collective-permute-start(f32[256,256]{1,0:T(8,128)S(1)} %get-tuple-element.1135), channel_id=1, source_target_pairs={{0,4},{4,8},{8,12},{12,16},{16,20},{20,24},{24,28},{1,5},{5,9},{9,... | collective-permute-start | bytes 786440 | tf_op jit(solution)/shard_map/while/body/eval_jaxpr/ppermute | solution.py:14
  353.8 5.6 %collective-permute-start.3 = (f32[256,256]{1,0:T(8,128)S(1)}, f32[256,256]{1,0:T(8,128)S(1)}, u32[]{:S(2)}, u32[]{:S(2)}) collective-permute-start(f32[256,256]{1,0:T(8,128)S(1)} %get-tuple-element.1137), channel_id=1, source_target_pairs={{4,0},{8,4},{12,8},{16,12},{20,16},{24,20},{28,24},{5,1},{9,5},{13... | collective-permute-start | bytes 786440 | tf_op jit(solution)/shard_map/while/body/eval_jaxpr/ppermute | solution.py:17
  367.9 14.4 %collective-permute-start = (f32[256,256]{1,0:T(8,128)S(1)}, f32[256,256]{1,0:T(8,128)S(1)}, u32[]{:S(2)}, u32[]{:S(2)}) collective-permute-start(f32[256,256]{1,0:T(8,128)S(1)} %get-tuple-element.1131), channel_id=1, source_target_pairs={{0,4},{4,8},{8,12},{12,16},{16,20},{20,24},{24,28},{1,5},{5,9},{9,... | collective-permute-start | bytes 786440 | tf_op jit(solution)/shard_map/while/body/eval_jaxpr/ppermute | solution.py:14
  402.5 9.5 %collective-permute-start.2 = (f32[256,256]{1,0:T(8,128)S(1)}, f32[256,256]{1,0:T(8,128)S(1)}, u32[]{:S(2)}, u32[]{:S(2)}) collective-permute-start(f32[256,256]{1,0:T(8,128)S(1)} %get-tuple-element.1135), channel_id=1, source_target_pairs={{0,4},{4,8},{8,12},{12,16},{16,20},{20,24},{24,28},{1,5},{5,9},{9,... | collective-permute-start | bytes 786440 | tf_op jit(solution)/shard_map/while/body/eval_jaxpr/ppermute | solution.py:14
  432.2 8.8 %collective-permute-start = (f32[256,256]{1,0:T(8,128)S(1)}, f32[256,256]{1,0:T(8,128)S(1)}, u32[]{:S(2)}, u32[]{:S(2)}) collective-permute-start(f32[256,256]{1,0:T(8,128)S(1)} %get-tuple-element.1131), channel_id=1, source_target_pairs={{0,4},{4,8},{8,12},{12,16},{16,20},{20,24},{24,28},{1,5},{5,9},{9,... | collective-permute-start | bytes 786440 | tf_op jit(solution)/shard_map/while/body/eval_jaxpr/ppermute | solution.py:14
  461.1 7.9 %collective-permute-start.2 = (f32[256,256]{1,0:T(8,128)S(1)}, f32[256,256]{1,0:T(8,128)S(1)}, u32[]{:S(2)}, u32[]{:S(2)}) collective-permute-start(f32[256,256]{1,0:T(8,128)S(1)} %get-tuple-element.1135), channel_id=1, source_target_pairs={{0,4},{4,8},{8,12},{12,16},{16,20},{20,24},{24,28},{1,5},{5,9},{9,... | collective-permute-start | bytes 786440 | tf_op jit(solution)/shard_map/while/body/eval_jaxpr/ppermute | solution.py:14
  496.1 10.3 %collective-permute-start.2 = (f32[256,256]{1,0:T(8,128)S(1)}, f32[256,256]{1,0:T(8,128)S(1)}, u32[]{:S(2)}, u32[]{:S(2)}) collective-permute-start(f32[256,256]{1,0:T(8,128)S(1)} %get-tuple-element.1135), channel_id=1, source_target_pairs={{0,4},{4,8},{8,12},{12,16},{16,20},{20,24},{24,28},{1,5},{5,9},{9,... | collective-permute-start | bytes 786440 | tf_op jit(solution)/shard_map/while/body/eval_jaxpr/ppermute | solution.py:14
  (19 other events, 140.5 us)
Sparse Core Ops, SparseCore 0:
  9.9 30.6 all-gather.4
  42.2 45.0 all-gather.2
where the time goes:
time: 525 us; the launch traced here: 520 us
  starting transfers between devices  194 us (37%)
  waiting for transfers between devices  191 us (36%)
  local copies, waits for them, and re-layouts  55.8 us (11%)
  other arithmetic  29 us (6%)
  loops' own time  20.4 us (4%)
  matrix products  16.1 us (3%)
  between operations  13.4 us (3%)
    ppermute x16, starting transfers between devices, extended_2(): lax.ppermute(lax.slice_in_dim(block, block.shape[dim] - width, None, axis...  173 us
    ppermute x16, waiting for transfers between devices, extended_2(): lax.ppermute(lax.slice_in_dim(block, 0, width, axis=dim), axis, backward)  96.3 us
    all_gather x1, waiting for transfers between devices, per_device(): lax.all_gather(reflector_vectors, 'col', axis=2, tiled=True)  46.6 us
    all_gather x1, waiting for transfers between devices, per_device(): lax.all_gather(reflector_factors, 'col', axis=2, tiled=True)  30.1 us
    dynamic_slice x16, other arithmetic, one_step(): lax.dynamic_slice(field_now, (0, col_start), (reflect, piece_cols))  28.5 us
    dynamic_update_slice x8, local copies, waits for them, and re-layouts, work(): lax.dynamic_update_slice_in_dim(field_in, extended[:row_dev], col_start, 1)  26.5 us
    ppermute x16, starting transfers between devices, extended_2(): lax.ppermute(lax.slice_in_dim(block, 0, width, axis=dim), axis, backward)  20.5 us
    another operation x8, loops' own time, work(): extended = lax.fori_loop(0, blocks_dev, one_block, extended)  18.4 us
  transfers between devices with their start and end apart: 34, of which 34 were waited for; matrix products, arithmetic and copies ran while one was open for 0% of the time, Pallas kernels for 0%

commit v1 on v0

v1 whole, which is shorter than its diff:
```python
import functools

import jax
import jax.numpy as jnp
from jax import lax
from jax.experimental import pallas as pl
from jax.experimental.pallas import tpu as pltpu
from jax.sharding import PartitionSpec as P

MESH = pl.DeviceIdType.MESH
f32, bf16 = jnp.float32, jnp.bfloat16
WIDTH = 128


def split(value):
    high = value.astype(bf16)
    return high, (value - high.astype(f32)).astype(bf16)


def dot3(a_high, a_low, b):
    b_high, b_low = split(b)
    dot = functools.partial(jnp.dot, preferred_element_type=f32)
    return dot(a_high, b_high) + (dot(a_high, b_low) + dot(a_low, b_high))


def kernel(
    count, x_ref, w_ref, out_ref,
    g_high, g_low, v_high, v_low, from_s0, from_s1, to_s0, to_s1, final,
    up_send, up_recv, down_send, down_recv,
):
    me = lax.axis_index("row")
    bw = g_high.shape[1]
    pieces, width = from_s0.shape[0], from_s0.shape[2]

    barrier = pltpu.get_barrier_semaphore()

    @pl.when(me > 0)
    def _():
        pl.semaphore_signal(barrier, inc=1, device_id={"row": me - 1}, device_id_type=MESH)

    @pl.when(me < count - 1)
    def _():
        pl.semaphore_signal(barrier, inc=1, device_id={"row": me + 1}, device_id_type=MESH)

    peers = jnp.where(me > 0, 1, 0) + jnp.where(me < count - 1, 1, 0)
    pl.semaphore_wait(barrier, peers)

    def prepare(k, carry):
        w_t = w_ref[k, :, : 2 * bw]
        f_high, f_low = split(w_ref[k, :, 2 * bw :])
        high, low = split(dot3(f_high, f_low, w_t))
        g_high[k], g_low[k] = high, low
        high, low = split(w_t.T)
        v_high[k], v_low[k] = high, low
        return carry

    lax.fori_loop(0, g_high.shape[0], prepare, 0)

    def apply(k, top, bottom):
        inner = dot3(g_high[k], g_low[k], jnp.concatenate([top, bottom], axis=0))
        change = dot3(v_high[k], v_low[k], inner)
        return top - change[:bw], bottom - change[bw:]

    def up(s, p):
        source, target = ((to_s0, from_s0), (to_s1, from_s1))[s]
        return pltpu.make_async_remote_copy(
            src_ref=source.at[p], dst_ref=target.at[p],
            send_sem=up_send.at[s, p], recv_sem=up_recv.at[s, p],
            device_id={"row": me - 1}, device_id_type=MESH,
        )

    def columns(p):
        return pl.ds(pl.multiple_of(p * width, width), width)

    def down(p):
        return pltpu.make_async_remote_copy(
            src_ref=final.at[p], dst_ref=out_ref.at[:, columns(p)],
            send_sem=down_send.at[p], recv_sem=down_recv.at[p],
            device_id={"row": me + 1}, device_id_type=MESH,
        )

    @pl.when(me == count - 1)
    def _():
        def piece(p, carry):
            x0, x1 = apply(1, x_ref[:bw, columns(p)], x_ref[bw:, columns(p)])
            to_s0[p] = x0
            up(0, p).start()
            to_s1[p] = x1
            up(1, p).start()
            return carry

        lax.fori_loop(0, pieces, piece, 0)

    @pl.when(me < count - 1)
    def _():
        def piece(p, carry):
            up(0, p).wait_recv()
            x1, b0 = apply(0, x_ref[bw:, columns(p)], from_s0[p])
            x0, x1 = apply(1, x_ref[:bw, columns(p)], x1)
            to_s0[p] = x0

            @pl.when(me > 0)
            def _():
                up(0, p).start()

            up(1, p).wait_recv()
            b0, b1 = apply(2, b0, from_s1[p])
            x1, b0 = apply(3, x1, b0)
            to_s1[p] = x1

            @pl.when(me > 0)
            def _():
                up(1, p).start()

            final[p, :bw] = b0
            final[p, bw:] = b1
            down(p).start()

            @pl.when(me == 0)
            def _():
                top, bottom = apply(4, to_s0[p], to_s1[p])
                out_ref[:bw, columns(p)] = top
                out_ref[bw:, columns(p)] = bottom

            return carry

        lax.fori_loop(0, pieces, piece, 0)

    def finish(p, carry):
        @pl.when(me > 0)
        def _():
            up(0, p).wait_send()
            up(1, p).wait_send()
            down(p).wait_recv()

        @pl.when(me < count - 1)
        def _():
            down(p).wait_send()

        return carry

    lax.fori_loop(0, pieces, finish, 0)


def per_device(singular_vectors, reflector_vectors, reflector_factors, sweep_bounds):
    count = lax.axis_size("row")
    me = lax.axis_index("row")
    rows, cols = singular_vectors.shape
    sweeps, blocks, _, span = reflector_vectors.shape
    bw = span // 2
    assert sweeps == 2 and blocks == 2 and rows == span and cols % WIDTH == 0
    pieces = cols // WIDTH

    both = jnp.concatenate([reflector_vectors, reflector_factors], axis=3)
    start = (me * blocks + jnp.arange(blocks)) * bw
    live = (start[None] >= sweep_bounds[:, :1]) & (start[None] <= sweep_bounds[:, 1:])
    is_factor = jnp.arange(span + bw) >= span
    both = jnp.where(live[:, :, None, None] | ~is_factor, both, 0.0)
    below = lax.ppermute(both[1, 0], "row", [(i + 1, i) for i in range(count - 1)])
    stack = jnp.stack([both[0, 1], both[0, 0], below, both[1, 1], both[1, 0]])
    weights = lax.all_gather(stack, "col", axis=1, tiled=True)

    n = weights.shape[0]
    piece = pltpu.VMEM((pieces, bw, WIDTH), f32)
    return pl.pallas_call(
        functools.partial(kernel, count),
        out_shape=jax.ShapeDtypeStruct((rows, cols), f32),
        in_specs=[pl.BlockSpec(memory_space=pltpu.VMEM)] * 2,
        out_specs=pl.BlockSpec(memory_space=pltpu.VMEM),
        scratch_shapes=[
            pltpu.VMEM((n, bw, span), bf16),
            pltpu.VMEM((n, bw, span), bf16),
            pltpu.VMEM((n, span, bw), bf16),
            pltpu.VMEM((n, span, bw), bf16),
            piece, piece, piece, piece,
            pltpu.VMEM((pieces, span, WIDTH), f32),
            pltpu.SemaphoreType.DMA((2, pieces)),
            pltpu.SemaphoreType.DMA((2, pieces)),
            pltpu.SemaphoreType.DMA((pieces,)),
            pltpu.SemaphoreType.DMA((pieces,)),
        ],
        compiler_params=pltpu.CompilerParams(
            collective_id=0, has_side_effects=True, vmem_limit_bytes=56 * 2**20
        ),
    )(singular_vectors, weights)


def solution(mesh):
    placed = (P("row", "col"), P(None, "row", "col", None), P(None, "row", "col", None), P())
    return jax.shard_map(
        per_device, mesh=mesh, in_specs=placed, out_specs=P("row", "col"), check_vma=False
    )
```

time: 525 us -> 188 us (0.36)
  starting transfers between devices: 194 us -> 1.29 us
  waiting for transfers between devices: 191 us -> 84.4 us
  Pallas kernels: 0 us -> 82.1 us
  local copies, waits for them, and re-layouts: 55.8 us -> 5.16 us
  other arithmetic: 29 us -> 1.37 us
  loops' own time: 20.4 us -> 0 us
  matrix products: 16.1 us -> 0 us
    ppermute x32 -> x1, starting transfers between devices: 194 us -> 1.29 us  [per_device(): lax.ppermute(both[1, 0], 'row', [(i + 1, i) for i in range(count - 1)])]
    ppermute x32 -> x1, waiting for transfers between devices: 114 us -> 1.99 us  [per_device(): lax.ppermute(both[1, 0], 'row', [(i + 1, i) for i in range(count - 1)])]
    pallas_call x0 -> x1, Pallas kernels: none -> 82.1 us  [per_device(): pl.pallas_call(functools.partial(kernel, count), out_shape=jax.ShapeDtype...]
    dynamic_slice x16 -> x0, other arithmetic: 28.5 us -> none  [one_step(): lax.dynamic_slice(field_now, (0, col_start), (reflect, piece_cols))]
    dynamic_update_slice x8 -> x0, local copies, waits for them, and re-layouts: 26.5 us -> none  [work(): lax.dynamic_update_slice_in_dim(field_in, extended[:row_dev], col_start, 1)]
    another operation x41 -> x0, loops' own time: 20.4 us -> none  [the longest x8 18.4 us: work(): extended = lax.fori_loop(0, blocks_dev, one_block, extended)]
    dot_general x24 -> x0, matrix products: 16.1 us -> none  [the longest x8 8.28 us: apply_block(): jnp.dot(vectors.T, inner_part, precision=exact_mode, preferred_element_ty...]
    dynamic_slice x16 -> x0, local copies, waits for them, and re-layouts: 14.9 us -> none  [the longest x8 10.5 us: work(): own_part = lax.dynamic_slice_in_dim(field_in, col_start, piece_cols, 1)]
  transfers between devices with their start and end apart: 34 -> 2, of which waited for: 34 -> 2; matrix products, arithmetic and copies ran while one was open for 0% -> 0% of each run, Pallas kernels for 0% -> 0%
where the time goes in v1:
time: 188 us
  waiting for transfers between devices  84.4 us (45%)
  Pallas kernels  82.1 us (44%)
  between operations  13.5 us (7%)
  local copies, waits for them, and re-layouts  5.16 us (3%)
    all_gather x1, waiting for transfers between devices, per_device(): weights = lax.all_gather(stack, 'col', axis=1, tiled=True)  82.4 us
    pallas_call x1, Pallas kernels, per_device(): pl.pallas_call(functools.partial(kernel, count), out_shape=jax.ShapeDtype...  82.1 us
    unnamed x7, local copies, waits for them, and re-layouts  4.16 us
  transfers between devices with their start and end apart: 2, of which 2 were waited for; matrix products, arithmetic and copies ran while one was open for 0% of the time, Pallas kernels for 0%

profile of v1, /device:TPU:0, one launch (start us, length us, event | category | flops | bytes accessed | tf_op | source)
XLA Modules:
  0.0 187.7 jit_solution(11780919346105659382)
XLA Ops:
  6.5 0.0 all-gather.2.cloned.1.call-start
  6.5 1.0 slice_reduce_fusion.1
  7.5 0.1 compare_and_fusion
  7.6 0.1 broadcast_or_fusion
  7.7 1.2 maximum_select_fusion
  8.9 1.3 collective-permute-start
  10.3 2.0 %collective-permute-done = f32[64,768]{1,0:T(8,128)S(1)} collective-permute-done((f32[64,768]{1,0:T(8,128)S(1)}, f32[64,768]{1,0:T(8,128)S(1)}, u32[]{:S(2)}, u32[]{:S(2)}) %collective-permute-start) | collective-permute-done | bytes 196640 | tf_op jit(solution)/shard_map/ppermute | solution.py:159
  12.3 0.0 copy-start
  12.3 0.9 copy-done
  13.3 0.0 all-gather.2.cloned.1.call-update
  13.3 82.4 %all-gather.2.cloned.1.call-done.w_ref = f32[5,256,768]{2,1,0:T(8,128)} async-done(((f32[5,64,768]{2,1,0:T(8,128)}), f32[5,256,768]{2,1,0:T(8,128)}) %all-gather.2.cloned.1.call-update) | async-done | bytes 3932176 | tf_op jit(solution)/shard_map/all_gather | solution.py:161
  95.7 82.1 %shard_map.46 = f32[512,1024]{1,0:T(8,128)} custom-call(f32[512,1024]{1,0:T(8,128)} %x_ref.1, f32[5,256,768]{2,1,0:T(8,128)} %all-gather.2.cloned.1.call-done.w_ref), custom_call_target="tpu_custom_call" | custom-call | tf_op jit(solution)/shard_map/pallas_call | solution.py:165
  177.7 3.2 %copy.10 = f32[512,1024]{1,0:T(8,128)} copy(f32[512,1024]{1,0:T(8,128)} %shard_map.46) | data formatting | bytes 4194304
  (8 shorter events, 0.1 us)
Async XLA Ops:
  6.5 89.1 %all-gather.2.cloned.1.call-start = ((), (), s32[]{:S(2)}) async-start(), calls=%async_computation | async-start | bytes 4915200 | tf_op jit(solution)/shard_map/all_gather | solution.py:161
  8.9 3.3 %collective-permute-start = (f32[64,768]{1,0:T(8,128)S(1)}, f32[64,768]{1,0:T(8,128)S(1)}, u32[]{:S(2)}, u32[]{:S(2)}) collective-permute-start(f32[64,768]{1,0:T(8,128)S(1)} %slice_bitcast_fusion.3), channel_id=1, source_target_pairs={{4,0},{8,4},{12,8},{16,12},{20,16},{24,20},{28,24},{5,1},{9,5},{13... | collective-permute-start | bytes 589832 | tf_op jit(solution)/shard_map/ppermute | solution.py:159
  12.3 0.9 copy-start
Sparse Core Ops, SparseCore 0:
  13.4 82.2 all-gather.1

commit v2 on v1

v2 whole, which is shorter than its diff:
```python
import functools

import jax
import jax.numpy as jnp
from jax import lax
from jax.experimental import pallas as pl
from jax.experimental.pallas import tpu as pltpu
from jax.sharding import PartitionSpec as P

MESH = pl.DeviceIdType.MESH
f32, bf16 = jnp.float32, jnp.bfloat16
WIDTH = 128


def split(value):
    high = value.astype(bf16)
    return high, (value - high.astype(f32)).astype(bf16)


def dot3(a, b):
    (a_high, a_low), (b_high, b_low) = a, b
    dot = functools.partial(jnp.dot, preferred_element_type=f32)
    return dot(a_high, b_high) + (dot(a_high, b_low) + dot(a_low, b_high))


def kernel(
    count, ring, bounds_ref, x_ref, vec_ref, fac_ref, out_ref,
    gathered, upper_high, upper_low, lower_high, lower_low,
    below, tops, returned, back, middle,
    hop_send, hop_recv, far_send, far_recv, up_send, up_recv, down_send, down_recv,
):
    me, slab = lax.axis_index("row"), lax.axis_index("col")
    bw = gathered.shape[2]
    part = bw // ring
    pieces, width = below.shape[1], below.shape[3]
    first, last = me == 0, me == count - 1

    def block_rows(owner):
        return pl.ds(pl.multiple_of(owner * part, part), part)

    for s in range(2):
        for b in range(2):
            w = vec_ref[s, b]
            gathered[s, b, block_rows(slab), :bw] = w[:, :bw] + w[:, bw:]
            gathered[s, b, block_rows(slab), bw:] = fac_ref[s, b]

    @pl.when(last)
    def _():
        below[...] = jnp.zeros_like(below)

    barrier = pltpu.get_barrier_semaphore()

    @pl.when(jnp.logical_not(first))
    def _():
        pl.semaphore_signal(barrier, inc=1, device_id={"row": me - 1}, device_id_type=MESH)

    @pl.when(jnp.logical_not(last))
    def _():
        pl.semaphore_signal(barrier, inc=1, device_id={"row": me + 1}, device_id_type=MESH)

    for k in range(1, ring):
        pl.semaphore_signal(
            barrier, inc=1, device_id={"col": lax.rem(slab + k, ring)}, device_id_type=MESH
        )
    peers = jnp.where(me > 0, 1, 0) + jnp.where(me < count - 1, 1, 0) + ring - 1
    pl.semaphore_wait(barrier, peers)

    def hop(way, t, owner):
        block = gathered.at[0, :, block_rows(owner)]
        return pltpu.make_async_remote_copy(
            src_ref=block, dst_ref=block,
            send_sem=hop_send.at[way, t], recv_sem=hop_recv.at[way, t],
            device_id={"col": slab + (1 - 2 * way)}, device_id_type=MESH,
        )

    def sends(way, t):
        if way == 0:
            return (slab - t >= 0) & (slab + 1 < ring)
        return (slab + t < ring) & (slab >= 1)

    def gets(way, t):
        return slab - 1 - t >= 0 if way == 0 else slab + 1 + t < ring

    for t in range(ring - 1):
        for way in range(2):
            sign = 1 - 2 * way

            @pl.when(sends(way, t))
            def _():
                hop(way, t, slab - sign * t).start()

        for way in range(2):
            sign = 1 - 2 * way

            @pl.when(gets(way, t))
            def _():
                hop(way, t, slab - sign * (t + 1)).wait_recv()

    def far(k, owner):
        block = gathered.at[1, :, block_rows(owner)]
        return pltpu.make_async_remote_copy(
            src_ref=block, dst_ref=block,
            send_sem=far_send.at[k], recv_sem=far_recv.at[k],
            device_id={"col": lax.rem(slab + k, ring)}, device_id_type=MESH,
        )

    for k in range(1, ring):
        far(k, slab).start()

    def build(s):
        row = lax.broadcasted_iota(jnp.int32, (bw, bw), 0)
        col = lax.broadcasted_iota(jnp.int32, (bw, bw), 1)
        row2 = lax.broadcasted_iota(jnp.int32, (2 * bw, 2 * bw), 0)
        col2 = lax.broadcasted_iota(jnp.int32, (2 * bw, 2 * bw), 1)
        unit = jnp.where(row2 == col2, 1.0, 0.0).astype(f32)

        def whole(b):
            start = (me * 2 + b) * bw
            live = (start >= bounds_ref[s, 0]) & (start <= bounds_ref[s, 1])
            packed = gathered[s, b, :, :bw]
            factor = gathered[s, b, :, bw:] * jnp.where(live, 1.0, 0.0).astype(f32)
            w_t = jnp.concatenate(
                [jnp.where(col >= row, packed, 0.0), jnp.where(col < row, packed, 0.0)], axis=1
            )
            g = dot3(split(factor), split(w_t))
            return unit - dot3(split(w_t.T), split(g))

        q1 = whole(1)
        lower_high[s], lower_low[s] = split(q1[bw:])
        q0 = whole(0)
        mixed = dot3(split(q0[:, bw:]), split(q1[:bw]))
        upper_high[s, :, :bw], upper_low[s, :, :bw] = split(q0[:, :bw])
        upper_high[s, :, bw:], upper_low[s, :, bw:] = split(mixed)

    def columns(p):
        return pl.ds(pl.multiple_of(p * width, width), width)

    def up(s, p):
        return pltpu.make_async_remote_copy(
            src_ref=tops.at[s, p], dst_ref=below.at[s, p],
            send_sem=up_send.at[s, p], recv_sem=up_recv.at[s, p],
            device_id={"row": me - 1}, device_id_type=MESH,
        )

    def down(s, p):
        target = back.at[p] if s == 0 else out_ref.at[pl.ds(0, bw), columns(p)]
        return pltpu.make_async_remote_copy(
            src_ref=returned.at[s, p], dst_ref=target,
            send_sem=down_send.at[s, p], recv_sem=down_recv.at[s, p],
            device_id={"row": me + 1}, device_id_type=MESH,
        )

    def sweep(s):
        def piece(p, carry):
            if s == 0:
                x0, x1 = x_ref[:bw, columns(p)], x_ref[bw:, columns(p)]
            else:
                @pl.when(jnp.logical_not(first))
                def _():
                    down(0, p).wait_recv()

                x0, x1 = back[p], middle[p]

            @pl.when(jnp.logical_not(last))
            def _():
                up(s, p).wait_recv()

            parts = split(jnp.concatenate([x0, x1, below[s, p]], axis=0))
            tops[s, p] = dot3((upper_high[s, :bw], upper_low[s, :bw]), parts)

            @pl.when(jnp.logical_not(first))
            def _():
                up(s, p).start()

            tail = tuple(value[bw:] for value in parts)
            returned[s, p] = dot3((lower_high[s], lower_low[s]), tail)

            @pl.when(jnp.logical_not(last))
            def _():
                down(s, p).start()

            kept = dot3((upper_high[s, bw:], upper_low[s, bw:]), parts)
            if s == 0:
                middle[p] = kept

                @pl.when(first)
                def _():
                    back[p] = tops[s, p]
            else:
                out_ref[bw:, columns(p)] = kept

                @pl.when(first)
                def _():
                    out_ref[:bw, columns(p)] = tops[s, p]

            return carry

        lax.fori_loop(0, pieces, piece, 0)

    build(0)
    sweep(0)
    for k in range(1, ring):
        far(k, lax.rem(slab + ring - k, ring)).wait_recv()
    build(1)
    sweep(1)

    for t in range(ring - 1):
        for way in range(2):
            @pl.when(sends(way, t))
            def _():
                hop(way, t, slab).wait_send()

    for k in range(1, ring):
        far(k, slab).wait_send()

    def finish(p, carry):
        @pl.when(jnp.logical_not(first))
        def _():
            up(0, p).wait_send()
            up(1, p).wait_send()
            down(1, p).wait_recv()

        @pl.when(jnp.logical_not(last))
        def _():
            down(0, p).wait_send()
            down(1, p).wait_send()

        return carry

    lax.fori_loop(0, pieces, finish, 0)


def per_device(singular_vectors, reflector_vectors, reflector_factors, sweep_bounds):
    count, ring = lax.axis_size("row"), lax.axis_size("col")
    rows, cols = singular_vectors.shape
    sweeps, blocks, _, span = reflector_vectors.shape
    bw = span // 2
    assert sweeps == 2 and blocks == 2 and rows == span and cols % WIDTH == 0
    pieces = cols // WIDTH
    vmem, dma = pltpu.VMEM, pltpu.SemaphoreType.DMA
    return pl.pallas_call(
        functools.partial(kernel, count, ring),
        out_shape=jax.ShapeDtypeStruct((rows, cols), f32),
        in_specs=[pl.BlockSpec(memory_space=pltpu.SMEM)] + [pl.BlockSpec(memory_space=vmem)] * 3,
        out_specs=pl.BlockSpec(memory_space=vmem),
        scratch_shapes=[
            vmem((2, 2, bw, span), f32),
            vmem((2, span, 3 * bw), bf16), vmem((2, span, 3 * bw), bf16),
            vmem((2, bw, span), bf16), vmem((2, bw, span), bf16),
            vmem((2, pieces, bw, WIDTH), f32),
            vmem((2, pieces, bw, WIDTH), f32),
            vmem((2, pieces, bw, WIDTH), f32),
            vmem((pieces, bw, WIDTH), f32),
            vmem((pieces, bw, WIDTH), f32),
            dma((2, ring)), dma((2, ring)), dma((ring,)), dma((ring,)),
            dma((2, pieces)), dma((2, pieces)), dma((2, pieces)), dma((2, pieces)),
        ],
        compiler_params=pltpu.CompilerParams(
            collective_id=0, has_side_effects=True, vmem_limit_bytes=56 * 2**20
        ),
    )(sweep_bounds, singular_vectors, reflector_vectors, reflector_factors)


def solution(mesh):
    placed = (P("row", "col"), P(None, "row", "col", None), P(None, "row", "col", None), P())
    return jax.shard_map(
        per_device, mesh=mesh, in_specs=placed, out_specs=P("row", "col"), check_vma=False
    )
```

time: 188 us -> 108 us (0.57)
  waiting for transfers between devices: 84.4 us -> 0 us
  Pallas kernels: 82.1 us -> 105 us
  between operations: 13.5 us -> 0.01 us
  local copies, waits for them, and re-layouts: 5.16 us -> 3.16 us
    all_gather x1 -> x0, waiting for transfers between devices: 82.4 us -> none  [per_device(): weights = lax.all_gather(stack, 'col', axis=1, tiled=True)]
    pallas_call x1, Pallas kernels: 82.1 us -> 105 us  [per_device(): pl.pallas_call(functools.partial(kernel, count, ring), out_shape=jax.Shap...]
    ppermute x1 -> x0, waiting for transfers between devices: 1.99 us -> none  [per_device(): lax.ppermute(both[1, 0], 'row', [(i + 1, i) for i in range(count - 1)])]
    unnamed x7 -> x1, local copies, waits for them, and re-layouts: 4.16 us -> 3.16 us
  transfers between devices with their start and end apart: 2 -> 0, of which waited for: 2 -> 0; matrix products, arithmetic and copies ran while one was open for 0% -> 0% of each run, Pallas kernels for 0% -> 0%
where the time goes in v2:
time: 108 us
  Pallas kernels  105 us (97%)
  local copies, waits for them, and re-layouts  3.16 us (3%)
    pallas_call x1, Pallas kernels, per_device(): pl.pallas_call(functools.partial(kernel, count, ring), out_shape=jax.Shap...  105 us
    unnamed x1, local copies, waits for them, and re-layouts  3.16 us

profile of v2, /device:TPU:0, one launch (start us, length us, event | category | flops | bytes accessed | tf_op | source)
XLA Modules:
  0.0 107.7 jit_solution(6515184779224235619)
XLA Ops:
  0.0 104.5 %shard_map.46 = f32[512,1024]{1,0:T(8,128)} custom-call(s32[2,2]{1,0:T(2,128)} %bounds_ref.1, f32[512,1024]{1,0:T(8,128)} %x_ref.1, f32[2,2,64,512]{3,2,1,0:T(8,128)} %vec_ref.1, f32[2,2,64,256]{3,2,1,0:T(8,128)} %fac_ref.1), custom_call_target="tpu_custom_call" | custom-call | tf_op jit(solution)/shard_map/pallas_call | solution.py:241
  104.5 3.2 %copy.6 = f32[512,1024]{1,0:T(8,128)} copy(f32[512,1024]{1,0:T(8,128)} %shard_map.46) | data formatting | bytes 4194304

commit v3 on v2

--- a/solution.py
+++ b/solution.py
@@ -27,7 +27,7 @@
     count, ring, bounds_ref, x_ref, vec_ref, fac_ref, out_ref,
     gathered, upper_high, upper_low, lower_high, lower_low,
     below, tops, returned, back, middle,
-    hop_send, hop_recv, far_send, far_recv, up_send, up_recv, down_send, down_recv,
+    hop_send, hop_recv, up_send, up_recv, down_send, down_recv,
 ):
     me, slab = lax.axis_index("row"), lax.axis_index("col")
     bw = gathered.shape[2]
@@ -58,18 +58,23 @@
     def _():
         pl.semaphore_signal(barrier, inc=1, device_id={"row": me + 1}, device_id_type=MESH)
 
-    for k in range(1, ring):
-        pl.semaphore_signal(
-            barrier, inc=1, device_id={"col": lax.rem(slab + k, ring)}, device_id_type=MESH
-        )
-    peers = jnp.where(me > 0, 1, 0) + jnp.where(me < count - 1, 1, 0) + ring - 1
+    @pl.when(slab > 0)
+    def _():
+        pl.semaphore_signal(barrier, inc=1, device_id={"col": slab - 1}, device_id_type=MESH)
+
+    @pl.when(slab < ring - 1)
+    def _():
+        pl.semaphore_signal(barrier, inc=1, device_id={"col": slab + 1}, device_id_type=MESH)
+
+    peers = jnp.where(me > 0, 1, 0) + jnp.where(me < count - 1, 1, 0)
+    peers = peers + jnp.where(slab > 0, 1, 0) + jnp.where(slab < ring - 1, 1, 0)
     pl.semaphore_wait(barrier, peers)
 
-    def hop(way, t, owner):
-        block = gathered.at[0, :, block_rows(owner)]
+    def hop(s, way, t, owner):
+        block = gathered.at[s, :, block_rows(owner)]
         return pltpu.make_async_remote_copy(
             src_ref=block, dst_ref=block,
-            send_sem=hop_send.at[way, t], recv_sem=hop_recv.at[way, t],
+            send_sem=hop_send.at[s, way, t], recv_sem=hop_recv.at[s, way, t],
             device_id={"col": slab + (1 - 2 * way)}, device_id_type=MESH,
         )
 
@@ -81,31 +86,23 @@
     def gets(way, t):
         return slab - 1 - t >= 0 if way == 0 else slab + 1 + t < ring
 
+    def start_hops(s, t):
+        for way in range(2):
+            @pl.when(sends(way, t))
+            def _():
+                hop(s, way, t, slab - (1 - 2 * way) * t).start()
+
+    def wait_hops(s, t):
+        for way in range(2):
+            @pl.when(gets(way, t))
+            def _():
+                hop(s, way, t, slab - (1 - 2 * way) * (t + 1)).wait_recv()
+
     for t in range(ring - 1):
-        for way in range(2):
-            sign = 1 - 2 * way
-
-            @pl.when(sends(way, t))
-            def _():
-                hop(way, t, slab - sign * t).start()
-
-        for way in range(2):
-            sign = 1 - 2 * way
-
-            @pl.when(gets(way, t))
-            def _():
-                hop(way, t, slab - sign * (t + 1)).wait_recv()
-
-    def far(k, owner):
-        block = gathered.at[1, :, block_rows(owner)]
-        return pltpu.make_async_remote_copy(
-            src_ref=block, dst_ref=block,
-            send_sem=far_send.at[k], recv_sem=far_recv.at[k],
-            device_id={"col": lax.rem(slab + k, ring)}, device_id_type=MESH,
-        )
-
-    for k in range(1, ring):
-        far(k, slab).start()
+        for s in range(2):
+            if t > 0:
+                wait_hops(s, t - 1)
+            start_hops(s, t)
 
     def build(s):
         row = lax.broadcasted_iota(jnp.int32, (bw, bw), 0)
@@ -197,10 +194,10 @@
 
         lax.fori_loop(0, pieces, piece, 0)
 
+    wait_hops(0, ring - 2)
     build(0)
     sweep(0)
-    for k in range(1, ring):
-        far(k, lax.rem(slab + ring - k, ring)).wait_recv()
+    wait_hops(1, ring - 2)
     build(1)
     sweep(1)
 
@@ -208,10 +205,8 @@
         for way in range(2):
             @pl.when(sends(way, t))
             def _():
-                hop(way, t, slab).wait_send()
-
-    for k in range(1, ring):
-        far(k, slab).wait_send()
+                hop(0, way, t, slab).wait_send()
+                hop(1, way, t, slab).wait_send()
 
     def finish(p, carry):
         @pl.when(jnp.logical_not(first))
@@ -252,7 +247,7 @@
             vmem((2, pieces, bw, WIDTH), f32),
             vmem((pieces, bw, WIDTH), f32),
             vmem((pieces, bw, WIDTH), f32),
-            dma((2, ring)), dma((2, ring)), dma((ring,)), dma((ring,)),
+            dma((2, 2, ring)), dma((2, 2, ring)),
             dma((2, pieces)), dma((2, pieces)), dma((2, pieces)), dma((2, pieces)),
         ],
         compiler_params=pltpu.CompilerParams(

time: 108 us -> 108 us (level)
  no operation moved by 1% of the time
where the time goes in v3:
time: 108 us
  Pallas kernels  105 us (97%)
  local copies, waits for them, and re-layouts  3.16 us (3%)
    pallas_call x1, Pallas kernels, per_device(): pl.pallas_call(functools.partial(kernel, count, ring), out_shape=jax.Shap...  105 us
    unnamed x1, local copies, waits for them, and re-layouts  3.16 us

profile of v3, /device:TPU:0, one launch (start us, length us, event | category | flops | bytes accessed | tf_op | source)
XLA Modules:
  0.0 107.9 jit_solution(11922467843123502492)
XLA Ops:
  0.0 104.8 %shard_map.46 = f32[512,1024]{1,0:T(8,128)} custom-call(s32[2,2]{1,0:T(2,128)} %bounds_ref.1, f32[512,1024]{1,0:T(8,128)} %x_ref.1, f32[2,2,64,512]{3,2,1,0:T(8,128)} %vec_ref.1, f32[2,2,64,256]{3,2,1,0:T(8,128)} %fac_ref.1), custom_call_target="tpu_custom_call" | custom-call | tf_op jit(solution)/shard_map/pallas_call | solution.py:236
  104.8 3.2 %copy.6 = f32[512,1024]{1,0:T(8,128)} copy(f32[512,1024]{1,0:T(8,128)} %shard_map.46) | data formatting | bytes 4194304
